TPU v7x, 32 devices: a whole 2x2x4 slice. The times are simulated.
32 devices in a mesh: seq: 16 (over z, x, core), row: 2 (over y).
Axes of the slice: x: 2, y: 2, z: 4, core: 2. Of those that a mesh axis runs over, the one named last changes fastest.
Arguments:
- patch_queries: bfloat16 [2048, 2048], P('seq', 'row'), may hold values from -15 to 15
- patch_keys: bfloat16 [2048, 2048], P('seq', 'row'), may hold values from -15 to 15
- patch_values: bfloat16 [2048, 2048], P('seq', 'row'), may hold values from -6 to 6
- patch_tasks: int32 [2048], P('seq'), may hold values from 0 to 7
- residual: bfloat16 [2048, 2048], P('seq', 'row'), may hold values from -6 to 6
- output_weight: bfloat16 [2048, 2048], P('row'), may hold values from -0.5 to 0.5
- global_down: bfloat16 [2048, 16], P('row'), may hold values from -0.5 to 0.5
- global_up: bfloat16 [16, 2048], P(None, 'row'), may hold values from -1.5 to 1.5
- global_scales: float32 [8, 16], replicated, may hold values from 0.25 to 4
- local_weight: bfloat16 [2048, 512], P('row'), may hold values from -0.125 to 0.125
- byte_ids: int32 [16384], P('seq'), may hold values from 0 to 255
- byte_table: bfloat16 [256, 512], replicated, may hold values from -6 to 6
- position_table: bfloat16 [8, 512], replicated, may hold values from -6 to 6
- norm_gain: float32 [512], replicated, may hold values from 0.5 to 1.5
- hidden_in: bfloat16 [2048, 512], P('row', 'seq'), may hold values from -0.25 to 0.25
- hidden_out: bfloat16 [2048, 512], P('row', 'seq'), may hold values from -0.125 to 0.125
- local_down: bfloat16 [512, 16], replicated, may hold values from -0.25 to 0.25
- local_up: bfloat16 [16, 2048], P(None, 'row'), may hold values from -1.5 to 1.5
- local_scales: float32 [8, 16], replicated, may hold values from 0.25 to 4
- cotangent: bfloat16 [16384, 512], P(('seq', 'row')), may hold values from -6 to 6
Outputs:
- grad_global_down: float32 [2048, 16], P('row')
- grad_global_up: float32 [16, 2048], P(None, 'row')
- grad_global_scales: float32 [8, 16], replicated
- grad_local_down: float32 [512, 16], replicated
- grad_local_up: float32 [16, 2048], P(None, 'row')
- grad_local_scales: float32 [8, 16], replicated
All inputs are finite; a program needn't handle non-finite values.
Results may differ from a plain program's by a relative error of at most 0.028.
Values may be sent and summed in bfloat16 or wider, within the bound.
A program may use at most 64 MiB of HBM per device.

v0:
```python
import math
import jax
import jax.numpy as jnp
from jax import lax
from jax.sharding import PartitionSpec as P

HEAD = 128
VOCAB = 256
PATCH = 8
TASKS = 8


def contract(left, right, left_dim, right_dim):
    return lax.dot_general(
        left, right, (((left_dim,), (right_dim,)), ((), ())), preferred_element_type=jnp.float32
    )


def select_rows(table, tasks):
    picks = (tasks[:, None] == jnp.arange(table.shape[0], dtype=jnp.int32)[None, :]).astype(
        jnp.float32
    )
    return jnp.dot(picks, table, precision=lax.Precision.HIGHEST)


def task_totals(tasks, values):
    picks = (tasks[:, None] == jnp.arange(TASKS, dtype=jnp.int32)[None, :]).astype(jnp.float32)
    return lax.dot_general(picks, values, (((0,), (0,)), ((), ())), precision=lax.Precision.HIGHEST)


def gelu_slope(upper):
    cumulative = 0.5 * (1.0 + lax.erf(upper * 0.7071067811865476))
    density = jnp.exp(-0.5 * upper * upper) * 0.3989422804014327
    return cumulative + upper * density


def local_inputs(
    identities, projected, tasks, byte_table, position_table, norm_gain, local_down, local_scales
):
    count = identities.shape[0]
    picks = (identities[:, None] == jnp.arange(VOCAB, dtype=jnp.int32)[None, :]).astype(
        jnp.bfloat16
    )
    embedded = jnp.dot(picks, byte_table, preferred_element_type=jnp.float32)
    patches = count // PATCH
    inputs = (
        embedded.reshape(patches, PATCH, -1)
        + position_table.astype(jnp.float32)[None]
        + projected.astype(jnp.float32)[:, None, :]
    )
    inputs = inputs.reshape(count, -1)
    inverse = lax.rsqrt(jnp.mean(inputs * inputs, axis=1, keepdims=True) + 1e-06)
    normed = (inputs * inverse * norm_gain).astype(jnp.bfloat16)
    lowered = jnp.dot(normed, local_down, preferred_element_type=jnp.float32)
    byte_tasks = jnp.repeat(tasks, PATCH)
    scales = select_rows(local_scales, byte_tasks)
    shrunk = (lowered * scales).astype(jnp.bfloat16)
    return (inputs, inverse, normed, lowered, scales, shrunk, byte_tasks)


def keep_state(current):
    return current


def update_state(state, query_rows, first, key_heads, value_heads, key_places, scale):
    running_max, running_sum, running_out = state
    count = query_rows.shape[0]
    heads = key_heads.shape[1]
    query_heads = query_rows.reshape(count, heads, HEAD)
    scores = (
        jnp.einsum("qhd,khd->hqk", query_heads, key_heads, preferred_element_type=jnp.float32)
        * scale
    )
    query_places = first + jnp.arange(count, dtype=jnp.int32)
    allowed = key_places[None, :] <= query_places[:, None]
    scores = jnp.where(allowed[None], scores, -1e30)
    new_max = jnp.maximum(running_max, jnp.max(scores, axis=2))
    weights = jnp.where(allowed[None], jnp.exp(scores - new_max[:, :, None]), 0.0)
    shrink = jnp.exp(running_max - new_max)
    running_sum = running_sum * shrink + jnp.sum(weights, axis=2)
    mixed = jnp.einsum(
        "hqk,khd->qhd",
        weights.astype(jnp.bfloat16),
        value_heads,
        preferred_element_type=jnp.float32,
    )
    running_out = running_out * jnp.transpose(shrink)[:, :, None] + mixed
    return (new_max, running_sum, running_out)


def finish_state(state):
    running_max, running_sum, running_out = state
    result = running_out / jnp.transpose(running_sum)[:, :, None]
    return result.reshape(result.shape[0], -1).astype(jnp.bfloat16)


def body(
    patch_queries,
    patch_keys,
    patch_values,
    patch_tasks,
    residual,
    output_weight,
    global_down,
    global_up,
    global_scales,
    local_weight,
    byte_ids,
    byte_table,
    position_table,
    norm_gain,
    hidden_in,
    hidden_out,
    local_down,
    local_up,
    local_scales,
    cotangent,
):
    rows = patch_queries.shape[0]
    width = patch_queries.shape[1]
    heads = width // HEAD
    row_count = lax.axis_size("row")
    seq_index = lax.axis_index("seq")
    row_index = lax.axis_index("row")
    scale = 1.0 / math.sqrt(HEAD)
    own_first = seq_index * rows
    groups = [(patch_queries, own_first)]

    def visit(state, query_rows, first, key_heads, value_heads, key_places):

        def refresh(current):
            return update_state(
                current, query_rows, first, key_heads, value_heads, key_places, scale
            )

        return lax.cond(
            key_places[0] <= first + query_rows.shape[0] - 1, refresh, keep_state, state
        )

    initial = tuple(
        (
            (
                jnp.full((heads, query_rows.shape[0]), -1e30, jnp.float32),
                jnp.zeros((heads, query_rows.shape[0]), jnp.float32),
                jnp.zeros((query_rows.shape[0], heads, HEAD), jnp.float32),
            )
            for query_rows, first in groups
        )
    )
    key_piece = lax.all_gather(patch_keys, "seq", axis=0, tiled=True)
    value_piece = lax.all_gather(patch_values, "seq", axis=0, tiled=True)
    count = key_piece.shape[0]
    span = math.gcd(count, 1024)

    def one_span(index, states):
        offset = index * span
        key_heads = lax.dynamic_slice_in_dim(key_piece, offset, span, 0).reshape(span, heads, HEAD)
        value_heads = lax.dynamic_slice_in_dim(value_piece, offset, span, 0).reshape(
            span, heads, HEAD
        )
        key_places = offset + jnp.arange(span, dtype=jnp.int32)
        updated = []
        for (query_rows, first), state in zip(groups, states):
            updated.append(visit(state, query_rows, first, key_heads, value_heads, key_places))
        return tuple(updated)

    states = lax.fori_loop(0, count // span, one_span, initial)
    outputs = [finish_state(state) for state in states]
    attended = outputs[0]
    reduced = lax.psum(jnp.dot(attended, global_down, preferred_element_type=jnp.float32), "row")
    task_scales = select_rows(global_scales, patch_tasks)
    scaled = (reduced * task_scales).astype(jnp.bfloat16)
    mixed = lax.psum_scatter(
        contract(output_weight, attended, 0, 1).astype(jnp.bfloat16),
        "row",
        scatter_dimension=0,
        tiled=True,
    ).astype(jnp.float32)
    mixed = mixed + jnp.transpose(residual.astype(jnp.float32)) + contract(global_up, scaled, 0, 1)
    mixed_b = mixed.astype(jnp.bfloat16)
    own_patches = rows // row_count
    own_bytes = own_patches * PATCH
    rows_in, rows_out = (
        lax.all_gather(hidden_in, "seq", axis=1, tiled=True),
        lax.all_gather(hidden_out, "seq", axis=1, tiled=True),
    )
    partial_value = contract(mixed_b, local_weight, 0, 0)
    projected = lax.psum(partial_value.astype(jnp.bfloat16), "row")
    every = local_inputs(
        byte_ids,
        projected,
        patch_tasks,
        byte_table,
        position_table,
        norm_gain,
        local_down,
        local_scales,
    )
    normed_all = every[2]
    shrunk_all = every[5]
    cotangent_all = lax.all_gather(cotangent, "row", axis=0, tiled=True)
    inputs, inverse, normed, lowered, scales, shrunk, byte_tasks = [
        lax.dynamic_slice_in_dim(value, row_index * own_bytes, own_bytes, 0) for value in every
    ]
    upper = contract(normed_all, rows_in, 1, 1) + jnp.dot(
        shrunk_all, local_up, preferred_element_type=jnp.float32
    )
    through = contract(cotangent_all, rows_out, 1, 1)
    grown = (through * gelu_slope(upper)).astype(jnp.bfloat16)
    grad_local_up = contract(shrunk_all, grown, 0, 0)
    back_norm, back_rank = (
        lax.psum_scatter(
            jnp.dot(grown, rows_in, preferred_element_type=jnp.float32).astype(jnp.bfloat16),
            "row",
            scatter_dimension=0,
            tiled=True,
        ).astype(jnp.float32),
        lax.psum_scatter(
            contract(grown, local_up, 1, 1).astype(jnp.bfloat16),
            "row",
            scatter_dimension=0,
            tiled=True,
        ).astype(jnp.float32),
    )
    grad_local_scales = task_totals(byte_tasks, back_rank * lowered)
    moved = (back_rank * scales).astype(jnp.bfloat16)
    grad_local_down = contract(normed, moved, 0, 0)
    back_total = back_norm + contract(moved, local_down, 1, 1)
    gained = back_total * norm_gain
    average = jnp.mean(gained * inputs, axis=1, keepdims=True)
    back_inputs = cotangent.astype(jnp.float32) + inverse * (
        gained - inputs * inverse * inverse * average
    )
    patch_grad = back_inputs.reshape(own_patches, PATCH, -1).sum(axis=1).astype(jnp.bfloat16)
    back_mixed = contract(
        lax.all_gather(patch_grad, "row", axis=0, tiled=True), local_weight, 1, 1
    ).astype(jnp.bfloat16)
    grad_global_up = contract(scaled, back_mixed, 0, 0)
    back_scaled = lax.psum(contract(back_mixed, global_up, 1, 1), "row")
    grad_global_scales = task_totals(patch_tasks, back_scaled * reduced)
    back_reduced = (back_scaled * task_scales).astype(jnp.bfloat16)
    grad_global_down = contract(attended, back_reduced, 0, 0)
    grad_global_down, grad_global_up, grad_global_scales, grad_local_up = lax.psum(
        (grad_global_down, grad_global_up, grad_global_scales, grad_local_up), "seq"
    )
    grad_local_down, grad_local_scales = lax.psum(
        (grad_local_down, grad_local_scales), ("seq", "row")
    )
    return (
        grad_global_down,
        grad_global_up,
        grad_global_scales,
        grad_local_down,
        grad_local_up,
        grad_local_scales,
    )


def solution(mesh):
    placed = (
        P("seq", "row"),
        P("seq", "row"),
        P("seq", "row"),
        P("seq"),
        P("seq", "row"),
        P("row", None),
        P("row", None),
        P(None, "row"),
        P(),
        P("row", None),
        P("seq"),
        P(),
        P(),
        P(),
        P("row", "seq"),
        P("row", "seq"),
        P(),
        P(None, "row"),
        P(),
        P(("seq", "row"), None),
    )
    return jax.shard_map(
        body,
        mesh=mesh,
        in_specs=placed,
        out_specs=(P("row", None), P(None, "row"), P(), P(), P(None, "row"), P()),
        check_vma=False,
    )
```

profile of v0, /device:TPU:0, one launch (start us, length us, event | category | flops | bytes accessed | tf_op | source)
XLA Modules:
  0.0 456.6 jit_solution(17964355863576185190)
XLA Ops:
  7.2 1.9 copy.32
  9.2 1.8 copy.33
  11.1 54.3 %all-gather.6.cloned.1.call-done = bf16[2048,1024]{0,1:T(8,128)(2,1)} async-done(((bf16[128,1024]{0,1:T(8,128)(2,1)}), bf16[2048,1024]{0,1:T(8,128)(2,1)}) %all-gather.6.cloned.1.call-update) | async-done | bytes 4194320 | tf_op jit(solution)/shard_map/all_gather | solution.py:150
  65.4 52.8 %all-gather.8.cloned.1.call-done = bf16[2048,1024]{0,1:T(8,128)(2,1)} async-done(((bf16[128,1024]{0,1:T(8,128)(2,1)}), bf16[2048,1024]{0,1:T(8,128)(2,1)}) %all-gather.8.cloned.1.call-update) | async-done | bytes 4194320 | tf_op jit(solution)/shard_map/all_gather | solution.py:151
  118.3 9.3 %while.19 = (s32[]{:T(128)}, f32[8,128]{1,0:T(8,128)S(1)}, f32[8,128]{1,0:T(8,128)S(1)}, f32[128,8,128]{2,0,1:T(8,128)S(1)}, s32[]{:T(128)}, /*index=5*/s32[]{:T...) while((s32[]{:T(128)}, f32[8,128]{1,0:T(8,128)S(1)}, ...), condition=%wide.region_5.6_spmd, body=%wide.region_0.5_spmd.sunk | while | flops 550899840 | bytes 28124504 | solution.py:167
  119.5 6.9 %conditional.2 = ((f32[8,128]{1,0:T(8,128)S(1)}, f32[8,128]{1,0:T(8,128)S(1)}, f32[128,8,128]{2,0,1:T(8,128)S(1)})) conditional(s32[]{:T(128)} %convert_element_type.155, (f32[8,128]{1,0:T(8,128)S(1)}, f32[8,128]{1,0:T(8,128)S(1)}, f32[128,8,128]{2,0,1:T(8,128)S(1)}) %tuple.65, (s32[1024]{0:T(1024)S(1)}, s32[]{:T(128)}, s32[]{:T(128)}, ...), branch_computations={%region_1.0_spmd, %region_2.4_spmd} | conditional | flops 550898816 | bytes 28120166 | solution.py:136
  119.5 2.7 constant_dynamic-slice_fusion
  122.5 1.1 fusion
  123.6 1.7 fusion.13
  125.3 1.0 fusion.2
  128.0 3.7 fusion.29
  133.1 5.0 %psum.63 = f32[128,16]{0,1:T(8,128)S(1)} all-reduce(f32[128,16]{0,1:T(8,128)S(1)} %fusion.65), channel_id=1, replica_groups=mesh['seq'=16,'row'=2] {'row'}, use_global_device_ids=true, to_apply=%region_7.8 | all-reduce | flops 2048 | bytes 16384 | tf_op jit(solution)/shard_map/psum | solution.py:170
  138.1 0.8 multiply_convert_fusion.3
  139.0 12.6 %reduce-scatter.4.cloned.1.call-done = bf16[1024,128]{0,1:T(8,128)(2,1)} async-done(((bf16[2048,128]{0,1:T(8,128)(2,1)}), bf16[1024,128]{0,1:T(8,128)(2,1)}) %reduce-scatter.4.cloned.1.call-update) | async-done | bytes 262160 | tf_op jit(solution)/shard_map/reduce_scatter | solution.py:173
  151.6 2.1 fusion.34
  153.7 0.7 all-gather.14.cloned.1.call-update
  155.2 19.1 %all-gather.10.cloned.1.call-done = bf16[1024,512]{1,0:T(8,128)(2,1)} async-done(((bf16[512,512]{1,0:T(8,128)(2,1)}), bf16[1024,512]{1,0:T(8,128)(2,1)}) %all-gather.10.cloned.1.call-update) | async-done | bytes 1048592 | tf_op jit(solution)/shard_map/all_gather | solution.py:201
  174.3 39.9 %all-gather.12.cloned.1.call-done = bf16[1024,512]{0,1:T(8,128)(2,1)} async-done(((bf16[1024,32]{0,1:T(8,128)(2,1)}), bf16[1024,512]{0,1:T(8,128)(2,1)}) %all-gather.12.cloned.1.call-update) | async-done | bytes 1048592 | tf_op jit(solution)/shard_map/all_gather | solution.py:185
  214.2 4.7 %fusion.60 = f32[1024,1024]{1,0:T(8,128)} fusion(bf16[1024,512]{1,0:T(8,128)(2,1)} %all-gather.10.cloned.1.call-done, bf16[1024,512]{0,1:T(8,128)(2,1)} %all-gather.12.cloned.1.call-done), kind=kOutput, calls=%fused_computation.86 | convolution fusion | flops 1073741824 | bytes 6291456 | tf_op jit(solution)/shard_map/dot_general | solution.py:14
  218.9 17.9 %all-reduce.5.cloned.1.call-done = bf16[128,512]{1,0:T(8,128)(2,1)} async-done(((bf16[128,512]{1,0:T(8,128)(2,1)}), bf16[128,512]{1,0:T(8,128)(2,1)}) %all-reduce.5.cloned.1.call-update) | async-done | bytes 131088 | tf_op jit(solution)/shard_map/psum | solution.py:188
  236.8 0.9 convert_element_type.97
  237.7 1.6 multiply_reduce_fusion
  239.4 0.6 copy-done.9
  240.2 1.0 copy-done.3
  241.2 1.0 multiply_convert_fusion.1
  242.3 34.6 %all-gather.14.cloned.1.call-done = bf16[1024,512]{0,1:T(8,128)(2,1)} async-done(((bf16[1024,32]{0,1:T(8,128)(2,1)}), bf16[1024,512]{0,1:T(8,128)(2,1)}) %all-gather.14.cloned.1.call-update) | async-done | bytes 1048592 | tf_op jit(solution)/shard_map/all_gather | solution.py:184
  276.8 2.9 fusion.61
  279.8 2.3 fusion.28
  282.1 1.3 copy-done.1
  283.4 1.3 convolution_convert_fusion.3
  284.9 4.1 convolution_convert_fusion.1
  289.2 1.3 dynamic_slice.47
  290.5 1.3 dynamic-slice.3
  291.8 2.6 fusion.64
  294.4 1.8 fusion.43
  296.2 1.2 fusion.36
  297.4 40.2 %all-reduce = (f32[512,16]{0,1:T(8,128)}, f32[8,16]{1,0:T(8,128)}) all-reduce(f32[512,16]{0,1:T(8,128)S(1)} %fusion.36, f32[8,16]{1,0:T(8,128)} %fusion.43), channel_id=1, replica_groups=mesh['seq'=16,'row'=2] {'seq','row'}, use_global_device_ids=true, to_apply=%region_18.19 | all-reduce | flops 8320 | bytes 66560 | tf_op jit(solution)/shard_map/psum | solution.py:246
  337.7 1.5 multiply_reduce_fusion.1
  339.2 1.6 bitcast_reduce_fusion
  340.8 5.2 %all_gather.23 = bf16[128,512]{1,0:T(8,128)(2,1)S(1)} all-gather(bf16[64,512]{1,0:T(8,128)(2,1)S(1)} %bitcast_reduce_fusion), channel_id=1, replica_groups=mesh['seq'=16,'row'=2] {'row'}, dimensions={0}, use_global_device_ids=true | all-gather | bytes 196608 | tf_op jit(solution)/shard_map/all_gather | solution.py:236
  346.7 0.8 fusion.63
  347.5 5.0 %psum.65 = f32[128,16]{0,1:T(8,128)S(1)} all-reduce(f32[128,16]{0,1:T(8,128)S(1)} %fusion.62), channel_id=1, replica_groups=mesh['seq'=16,'row'=2] {'row'}, use_global_device_ids=true, to_apply=%region_14.15 | all-reduce | flops 2048 | bytes 16384 | tf_op jit(solution)/shard_map/psum | solution.py:239
  352.4 0.8 fusion.55
  353.5 30.1 %psum.68 = f32[8,16]{1,0:T(8,128)} all-reduce(f32[8,16]{1,0:T(8,128)S(1)} %fusion.49), channel_id=1, replica_groups=mesh['seq'=16,'row'=2] {'seq'}, use_global_device_ids=true, to_apply=%region_17.18 | all-reduce | flops 128 | bytes 1024 | tf_op jit(solution)/shard_map/psum | solution.py:243
  383.6 61.7 %all-reduce.7.cloned.1.call-done = (f32[1024,16]{0,1:T(8,128)}, f32[16,1024]{1,0:T(8,128)}, f32[16,1024]{1,0:T(8,128)}) async-done(((f32[1024,16]{0,1:T(8,128)}, f32[16,1024]{1,0:T(8,128)}, f32[16,1024]{1,0:T(8,128)}), (f32[1024,16]{0,1:T(8,128)}, f32[16,1024]{1,0:T(8,128)}, f32[16,1024]{1,0:T(8,128)})) %all-reduce.7.cloned.1.call-update) | async-done | bytes 196624 | tf_op jit(solution)/shard_map/psum | solution.py:243
  445.3 1.5 copy.67
  446.8 1.5 copy.68
  448.3 1.5 copy.69
  (90 shorter events, 5.4 us)
Async XLA Ops:
  7.2 144.4 %copy-start = (bf16[1024,512]{1,0:T(8,128)(2,1)S(1)}, bf16[1024,512]{1,0:T(8,128)(2,1)}, u32[]{:S(2)}) copy-start(bf16[1024,512]{1,0:T(8,128)(2,1)} %param.33) | copy-start | bytes 3145732
  7.2 58.2 %all-gather.6.cloned.1.call-start = ((), (), s32[]{:S(2)}) async-start(), calls=%async_computation.3 | async-start | bytes 4456448 | tf_op jit(solution)/shard_map/all_gather | solution.py:150
  9.1 109.1 %all-gather.8.cloned.1.call-start = ((), (), s32[]{:S(2)}) async-start(), calls=%async_computation.4 | async-start | bytes 4456448 | tf_op jit(solution)/shard_map/all_gather | solution.py:151
  11.0 140.6 %reduce-scatter.4.cloned.1.call-start = ((), (), s32[]{:S(2)}) async-start(), calls=%async_computation.5 | async-start | bytes 786432 | tf_op jit(solution)/shard_map/reduce_scatter | solution.py:173
  119.5 3.0 copy-start.2
  127.6 5.3 %copy-start.8 = (bf16[1024,16]{0,1:T(8,128)(2,1)S(1)}, bf16[1024,16]{0,1:T(8,128)(2,1)}, u32[]{:S(2)}) copy-start(bf16[1024,16]{0,1:T(8,128)(2,1)} %param.30) | copy-start | bytes 98308
  127.6 10.5 %copy-start.18 = (s32[128]{0:T(128)S(1)}, s32[128]{0:T(128)}, u32[]{:S(2)}) copy-start(s32[128]{0:T(128)} %param.27) | copy-start | bytes 1540
  127.6 10.5 %copy-start.20 = (f32[8,16]{1,0:T(8,128)S(1)}, f32[8,16]{1,0:T(8,128)}, u32[]{:S(2)}) copy-start(f32[8,16]{1,0:T(8,128)} %param.32) | copy-start | bytes 1540
  127.7 23.9 %copy-start.4 = (bf16[128,1024]{1,0:T(8,128)(2,1)S(1)}, bf16[128,1024]{1,0:T(8,128)(2,1)}, u32[]{:S(2)}) copy-start(bf16[128,1024]{1,0:T(8,128)(2,1)} %param.28) | copy-start | bytes 786436
  127.7 23.9 %copy-start.5 = (bf16[16,1024]{1,0:T(8,128)(2,1)S(1)}, bf16[16,1024]{1,0:T(8,128)(2,1)}, u32[]{:S(2)}) copy-start(bf16[16,1024]{1,0:T(8,128)(2,1)} %param.31) | copy-start | bytes 98308
  127.9 26.5 %copy-start.13 = (bf16[8,512]{1,0:T(8,128)(2,1)S(1)}, bf16[8,512]{1,0:T(8,128)(2,1)}, u32[]{:S(2)}) copy-start(bf16[8,512]{1,0:T(8,128)(2,1)} %param.36) | copy-start | bytes 24580
  128.0 26.7 %copy-start.21 = (f32[8,16]{1,0:T(8,128)S(1)}, f32[8,16]{1,0:T(8,128)}, u32[]{:S(2)}) copy-start(f32[8,16]{1,0:T(8,128)} %param.42) | copy-start | bytes 1540
  131.7 42.6 %all-gather.10.cloned.1.call-start = ((), (), s32[]{:S(2)}) async-start(), calls=%async_computation.7 | async-start | bytes 1572864 | tf_op jit(solution)/shard_map/all_gather | solution.py:201
  132.3 81.9 %all-gather.12.cloned.1.call-start = ((), (), s32[]{:S(2)}) async-start(), calls=%async_computation.8 | async-start | bytes 1114112 | tf_op jit(solution)/shard_map/all_gather | solution.py:185
  132.9 103.9 %all-reduce.5.cloned.1.call-start = ((), (), s32[]{:S(2)}) async-start(), calls=%async_computation.6 | async-start | bytes 262144 | tf_op jit(solution)/shard_map/psum | solution.py:188
  138.1 80.8 %copy-start.15 = (f32[128,16]{0,1:T(8,128)}, f32[128,16]{0,1:T(8,128)S(1)}, u32[]{:S(2)}) copy-start(f32[128,16]{0,1:T(8,128)S(1)} %psum.63) | copy-start | bytes 24580
  139.0 15.6 %copy-start.10 = (bf16[128,16]{0,1:T(8,128)(2,1)}, bf16[128,16]{0,1:T(8,128)(2,1)S(1)}, u32[]{:S(2)}) copy-start(bf16[128,16]{0,1:T(8,128)(2,1)S(1)} %get-tuple-element.359) | copy-start | bytes 12292
  153.7 123.2 %all-gather.14.cloned.1.call-start = ((), (), s32[]{:S(2)}) async-start(), calls=%async_computation.9 | async-start | bytes 1114112 | tf_op jit(solution)/shard_map/all_gather | solution.py:184
  154.4 140.0 %reduce-scatter.8.cloned.1.call-start = ((), (), s32[]{:S(2)}) async-start(), calls=%async_computation.11 | async-start | bytes 49152 | tf_op jit(solution)/shard_map/reduce_scatter | solution.py:218
  154.7 64.2 %copy-start.12 = (s32[1024]{0:T(1024)}, s32[1024]{0:T(1024)S(1)}, u32[]{:S(2)}) copy-start(s32[1024]{0:T(1024)S(1)} %eq.32) | copy-start | bytes 12292
  155.2 84.8 %copy-start.17 = (f32[512]{0:T(512)S(1)}, f32[512]{0:T(512)}, u32[]{:S(2)}) copy-start(f32[512]{0:T(512)} %param.37) | copy-start | bytes 6148
  218.9 22.3 %copy-start.6 = (bf16[512,16]{0,1:T(8,128)(2,1)S(1)}, bf16[512,16]{0,1:T(8,128)(2,1)}, u32[]{:S(2)}) copy-start(bf16[512,16]{0,1:T(8,128)(2,1)} %param.40) | copy-start | bytes 49156
  239.4 0.6 copy-start.9
  240.2 1.0 copy-start.3
  276.8 3.0 copy-start.7
  276.8 3.0 copy-start.22
  282.1 1.3 copy-start.1
  284.7 52.9 %reduce-scatter.6.cloned.1.call-start = ((), (), s32[]{:S(2)}) async-start(), calls=%async_computation.10 | async-start | bytes 1572864 | tf_op jit(solution)/shard_map/reduce_scatter | solution.py:212
  289.1 156.2 %all-reduce.7.cloned.1.call-start = ((), (), s32[]{:S(2)}) async-start(), calls=%async_computation.12 | async-start | bytes 393216 | tf_op jit(solution)/shard_map/psum | solution.py:243
  337.6 9.0 %copy-start.11 = (bf16[128,16]{0,1:T(8,128)(2,1)S(1)}, bf16[128,16]{0,1:T(8,128)(2,1)}, u32[]{:S(2)}) copy-start(bf16[128,16]{0,1:T(8,128)(2,1)} %copy-done.10) | copy-start | bytes 12292
  337.6 14.8 %copy-start.14 = (f32[128,16]{0,1:T(8,128)S(1)}, f32[128,16]{0,1:T(8,128)}, u32[]{:S(2)}) copy-start(f32[128,16]{0,1:T(8,128)} %get-tuple-element.360) | copy-start | bytes 24580
  337.6 15.7 %copy-start.16 = (f32[128,16]{0,1:T(8,128)S(1)}, f32[128,16]{0,1:T(8,128)}, u32[]{:S(2)}) copy-start(f32[128,16]{0,1:T(8,128)} %copy-done.15) | copy-start | bytes 24580
  337.6 15.7 %copy-start.19 = (s32[128]{0:T(128)S(1)}, s32[128]{0:T(128)}, u32[]{:S(2)}) copy-start(s32[128]{0:T(128)} %param.27) | copy-start | bytes 1540
Sparse Core Ops, SparseCore 0:
  10.1 55.1 all-gather.5
  67.5 50.6 all-gather.7
  131.9 19.6 reduce-scatter.3
  153.0 21.2 all-gather.9
  176.3 37.8 all-gather.11
  216.3 20.4 all-reduce.4
  239.0 37.8 all-gather.13
  284.8 8.9 reduce-scatter.7
  296.1 20.9 reduce-scatter.5
  353.4 91.8 all-reduce.6
where the time goes:
time: 457 us
  waiting for transfers between devices  295 us (65%)
  blocking collectives  85.4 us (19%)
  matrix products  37.7 us (8%)
  local copies, waits for them, and re-layouts  17.9 us (4%)
  between operations  14.5 us (3%)
    psum x1, waiting for transfers between devices, body(): lax.psum((grad_global_down, grad_global_up, grad_global_scales, grad_loca...  61.7 us
    all_gather x1, waiting for transfers between devices, body(): key_piece = lax.all_gather(patch_keys, 'seq', axis=0, tiled=True)  54.3 us
    all_gather x1, waiting for transfers between devices, body(): value_piece = lax.all_gather(patch_values, 'seq', axis=0, tiled=True)  52.8 us
    psum x1, blocking collectives, body(): lax.psum((grad_local_down, grad_local_scales), ('seq', 'row'))  40.2 us
    all_gather x1, waiting for transfers between devices, body(): lax.all_gather(hidden_out, 'seq', axis=1, tiled=True)  39.9 us
    all_gather x1, waiting for transfers between devices, body(): lax.all_gather(hidden_in, 'seq', axis=1, tiled=True)  34.6 us
    psum x1, blocking collectives, body(): lax.psum((grad_global_down, grad_global_up, grad_global_scales, grad_loca...  30.1 us
    dot_general x12, matrix products, contract(): lax.dot_general(left, right, (((left_dim,), (right_dim,)), ((), ())), pre...  22.4 us
  transfers between devices with their start and end apart: 10, of which 8 were waited for; matrix products, arithmetic and copies ran while one was open for 6% of the time, Pallas kernels for 0%

commit v1 on v0

--- a/solution.py
+++ b/solution.py
@@ -243,9 +243,12 @@
     grad_global_down, grad_global_up, grad_global_scales, grad_local_up = lax.psum(
         (grad_global_down, grad_global_up, grad_global_scales, grad_local_up), "seq"
     )
-    grad_local_down, grad_local_scales = lax.psum(
-        (grad_local_down, grad_local_scales), ("seq", "row")
-    )
+
+    def see_results_in(x_part):
+        seen_now = lax.psum(x_part, axis_name="row")
+        return lax.psum(seen_now, axis_name="seq")
+
+    grad_local_down, grad_local_scales = see_results_in((grad_local_down, grad_local_scales))
     return (
         grad_global_down,
         grad_global_up,

time: 457 us -> 439 us (0.961)
  blocking collectives: 85.4 us -> 76 us
  waiting for transfers between devices: 295 us -> 286 us
    psum x1 -> x0, blocking collectives: 40.2 us -> none  [body(): lax.psum((grad_local_down, grad_local_scales), ('seq', 'row'))]
    psum x1, blocking collectives: 30.1 us -> 58.6 us  [body(): lax.psum((grad_global_down, grad_global_up, grad_global_scales, grad_loca...]
    psum x1, waiting for transfers between devices: 61.7 us -> 34 us  [body(): lax.psum((grad_global_down, grad_global_up, grad_global_scales, grad_loca...]
    reduce_scatter x1, waiting for transfers between devices: 0.02 us -> 19.1 us  [body(): lax.psum_scatter(jnp.dot(grown, rows_in, preferred_element_type=jnp.float...]
    unnamed x49 -> x51, local copies, waits for them, and re-layouts: 11.1 us -> 11.1 us
  transfers between devices with their start and end apart: 10 -> 10, of which waited for: 8 -> 9; matrix products, arithmetic and copies ran while one was open for 6% -> 6% of each run, Pallas kernels for 0% -> 0%
where the time goes in v1:
time: 439 us
  waiting for transfers between devices  286 us (65%)
  blocking collectives  76 us (17%)
  matrix products  37.8 us (9%)
  local copies, waits for them, and re-layouts  18 us (4%)
  between operations  14.5 us (3%)
    psum x1, blocking collectives, body(): lax.psum((grad_global_down, grad_global_up, grad_global_scales, grad_loca...  58.6 us
    all_gather x1, waiting for transfers between devices, body(): key_piece = lax.all_gather(patch_keys, 'seq', axis=0, tiled=True)  54.3 us
    all_gather x1, waiting for transfers between devices, body(): value_piece = lax.all_gather(patch_values, 'seq', axis=0, tiled=True)  52.8 us
    all_gather x1, waiting for transfers between devices, body(): lax.all_gather(hidden_out, 'seq', axis=1, tiled=True)  39.9 us
    all_gather x1, waiting for transfers between devices, body(): lax.all_gather(hidden_in, 'seq', axis=1, tiled=True)  34.6 us
    psum x1, waiting for transfers between devices, body(): lax.psum((grad_global_down, grad_global_up, grad_global_scales, grad_loca...  34 us
    dot_general x12, matrix products, contract(): lax.dot_general(left, right, (((left_dim,), (right_dim,)), ((), ())), pre...  22.4 us
    all_gather x1, waiting for transfers between devices, body(): cotangent_all = lax.all_gather(cotangent, 'row', axis=0, tiled=True)  19.1 us
  transfers between devices with their start and end apart: 10, of which 9 were waited for; matrix products, arithmetic and copies ran while one was open for 6% of the time, Pallas kernels for 0%

profile of v1, /device:TPU:0, one launch (start us, length us, event | category | flops | bytes accessed | tf_op | source)
XLA Modules:
  0.0 438.6 jit_solution(9618418370625930633)
XLA Ops:
  7.2 1.9 copy.32
  9.2 1.8 copy.33
  11.1 54.3 %all-gather.6.cloned.1.call-done = bf16[2048,1024]{0,1:T(8,128)(2,1)} async-done(((bf16[128,1024]{0,1:T(8,128)(2,1)}), bf16[2048,1024]{0,1:T(8,128)(2,1)}) %all-gather.6.cloned.1.call-update) | async-done | bytes 4194320 | tf_op jit(solution)/shard_map/all_gather | solution.py:150
  65.4 52.8 %all-gather.8.cloned.1.call-done = bf16[2048,1024]{0,1:T(8,128)(2,1)} async-done(((bf16[128,1024]{0,1:T(8,128)(2,1)}), bf16[2048,1024]{0,1:T(8,128)(2,1)}) %all-gather.8.cloned.1.call-update) | async-done | bytes 4194320 | tf_op jit(solution)/shard_map/all_gather | solution.py:151
  118.3 9.3 %while.19 = (s32[]{:T(128)}, f32[8,128]{1,0:T(8,128)S(1)}, f32[8,128]{1,0:T(8,128)S(1)}, f32[128,8,128]{2,0,1:T(8,128)S(1)}, s32[]{:T(128)}, /*index=5*/s32[]{:T...) while((s32[]{:T(128)}, f32[8,128]{1,0:T(8,128)S(1)}, ...), condition=%wide.region_5.6_spmd, body=%wide.region_0.5_spmd.sunk | while | flops 550899840 | bytes 28124504 | solution.py:167
  119.5 6.9 %conditional.2 = ((f32[8,128]{1,0:T(8,128)S(1)}, f32[8,128]{1,0:T(8,128)S(1)}, f32[128,8,128]{2,0,1:T(8,128)S(1)})) conditional(s32[]{:T(128)} %convert_element_type.155, (f32[8,128]{1,0:T(8,128)S(1)}, f32[8,128]{1,0:T(8,128)S(1)}, f32[128,8,128]{2,0,1:T(8,128)S(1)}) %tuple.65, (s32[1024]{0:T(1024)S(1)}, s32[]{:T(128)}, s32[]{:T(128)}, ...), branch_computations={%region_1.0_spmd, %region_2.4_spmd} | conditional | flops 550898816 | bytes 28120166 | solution.py:136
  119.5 2.7 constant_dynamic-slice_fusion
  122.5 1.1 fusion
  123.6 1.7 fusion.13
  125.3 1.0 fusion.2
  128.0 3.8 fusion.29
  133.1 5.0 %psum.77 = f32[128,16]{0,1:T(8,128)S(1)} all-reduce(f32[128,16]{0,1:T(8,128)S(1)} %fusion.65), channel_id=1, replica_groups=mesh['seq'=16,'row'=2] {'row'}, use_global_device_ids=true, to_apply=%region_7.8 | all-reduce | flops 2048 | bytes 16384 | tf_op jit(solution)/shard_map/psum | solution.py:170
  138.1 0.9 multiply_convert_fusion.3
  139.0 12.6 %reduce-scatter.4.cloned.1.call-done = bf16[1024,128]{0,1:T(8,128)(2,1)} async-done(((bf16[2048,128]{0,1:T(8,128)(2,1)}), bf16[1024,128]{0,1:T(8,128)(2,1)}) %reduce-scatter.4.cloned.1.call-update) | async-done | bytes 262160 | tf_op jit(solution)/shard_map/reduce_scatter | solution.py:173
  151.6 2.1 fusion.34
  153.7 0.7 all-gather.14.cloned.1.call-update
  155.2 19.1 %all-gather.10.cloned.1.call-done = bf16[1024,512]{1,0:T(8,128)(2,1)} async-done(((bf16[512,512]{1,0:T(8,128)(2,1)}), bf16[1024,512]{1,0:T(8,128)(2,1)}) %all-gather.10.cloned.1.call-update) | async-done | bytes 1048592 | tf_op jit(solution)/shard_map/all_gather | solution.py:201
  174.3 39.9 %all-gather.12.cloned.1.call-done = bf16[1024,512]{0,1:T(8,128)(2,1)} async-done(((bf16[1024,32]{0,1:T(8,128)(2,1)}), bf16[1024,512]{0,1:T(8,128)(2,1)}) %all-gather.12.cloned.1.call-update) | async-done | bytes 1048592 | tf_op jit(solution)/shard_map/all_gather | solution.py:185
  214.2 4.7 %fusion.60 = f32[1024,1024]{1,0:T(8,128)} fusion(bf16[1024,512]{1,0:T(8,128)(2,1)} %all-gather.10.cloned.1.call-done, bf16[1024,512]{0,1:T(8,128)(2,1)} %all-gather.12.cloned.1.call-done), kind=kOutput, calls=%fused_computation.86 | convolution fusion | flops 1073741824 | bytes 6291456 | tf_op jit(solution)/shard_map/dot_general | solution.py:14
  218.9 17.9 %all-reduce.6.cloned.1.call-done = bf16[128,512]{1,0:T(8,128)(2,1)} async-done(((bf16[128,512]{1,0:T(8,128)(2,1)}), bf16[128,512]{1,0:T(8,128)(2,1)}) %all-reduce.6.cloned.1.call-update) | async-done | bytes 131088 | tf_op jit(solution)/shard_map/psum | solution.py:188
  236.8 0.9 convert_element_type.97
  237.8 1.6 multiply_reduce_fusion
  239.4 0.6 copy-done.9
  240.3 1.0 copy-done.3
  241.2 1.0 multiply_convert_fusion.1
  242.3 34.6 %all-gather.14.cloned.1.call-done = bf16[1024,512]{0,1:T(8,128)(2,1)} async-done(((bf16[1024,32]{0,1:T(8,128)(2,1)}), bf16[1024,512]{0,1:T(8,128)(2,1)}) %all-gather.14.cloned.1.call-update) | async-done | bytes 1048592 | tf_op jit(solution)/shard_map/all_gather | solution.py:184
  276.9 2.9 fusion.61
  279.8 2.3 fusion.28
  282.1 1.3 copy-done.1
  283.5 1.3 convolution_convert_fusion.3
  285.0 4.1 convolution_convert_fusion.1
  289.2 1.3 dynamic_slice.47
  290.5 1.3 dynamic-slice.3
  291.9 2.6 fusion.64
  294.5 1.8 fusion.43
  296.2 1.2 fusion.36
  297.5 19.1 %reduce-scatter.6.cloned.1.call-done = bf16[512,512]{1,0:T(8,128)(2,1)} async-done(((bf16[1024,512]{1,0:T(8,128)(2,1)}), bf16[512,512]{1,0:T(8,128)(2,1)}) %reduce-scatter.6.cloned.1.call-update) | async-done | bytes 524304 | tf_op jit(solution)/shard_map/reduce_scatter | solution.py:212
  316.5 1.5 multiply_reduce_fusion.1
  318.1 1.6 bitcast_reduce_fusion
  319.7 4.9 %all_gather.23 = bf16[128,512]{1,0:T(8,128)(2,1)S(1)} all-gather(bf16[64,512]{1,0:T(8,128)(2,1)S(1)} %bitcast_reduce_fusion), channel_id=1, replica_groups=mesh['seq'=16,'row'=2] {'row'}, dimensions={0}, use_global_device_ids=true | all-gather | bytes 196608 | tf_op jit(solution)/shard_map/all_gather | solution.py:236
  325.3 0.8 fusion.63
  326.1 7.5 %all-reduce.2 = (f32[128,16]{0,1:T(8,128)S(1)}, f32[512,16]{0,1:T(8,128)S(1)}, f32[8,16]{1,0:T(8,128)S(1)}) all-reduce(f32[128,16]{0,1:T(8,128)S(1)} %fusion.62, f32[512,16]{0,1:T(8,128)S(1)} %fusion.36, f32[8,16]{1,0:T(8,128)S(1)} %copy-done.18), channel_id=1, replica_groups=mesh['seq'=16,'row'=2] {'row'}, use_global_device_ids=true, to_apply=%region_14.15 | all-reduce | flops 10368 | bytes 82944 | tf_op jit(solution)/shard_map/psum | solution.py:239
  333.7 0.8 fusion.55
  334.8 58.6 %all-reduce = (f32[8,16]{1,0:T(8,128)}, f32[512,16]{0,1:T(8,128)}, f32[8,16]{1,0:T(8,128)}) all-reduce(f32[8,16]{1,0:T(8,128)S(1)} %fusion.49, f32[512,16]{0,1:T(8,128)S(1)} %get-tuple-element.355, f32[8,16]{1,0:T(8,128)S(1)} %get-tuple-element.356), channel_id=1, replica_groups=mesh['seq'=16,'row'=2] {'seq'}, use_global_device_ids=true, to_apply=%region_17.18 | all-reduce | flops 8448 | bytes 67584 | tf_op jit(solution)/shard_map/psum | solution.py:243
  393.4 34.0 %all-reduce.8.cloned.1.call-done = (f32[1024,16]{0,1:T(8,128)}, f32[16,1024]{1,0:T(8,128)}, f32[16,1024]{1,0:T(8,128)}) async-done(((f32[1024,16]{0,1:T(8,128)}, f32[16,1024]{1,0:T(8,128)}, f32[16,1024]{1,0:T(8,128)}), (f32[1024,16]{0,1:T(8,128)}, f32[16,1024]{1,0:T(8,128)}, f32[16,1024]{1,0:T(8,128)})) %all-reduce.8.cloned.1.call-update) | async-done | bytes 196624 | tf_op jit(solution)/shard_map/psum | solution.py:243
  427.3 1.5 copy.67
  428.8 1.5 copy.68
  430.3 1.5 copy.69
  (91 shorter events, 5.4 us)
Async XLA Ops:
  7.2 144.4 %copy-start = (bf16[1024,512]{1,0:T(8,128)(2,1)S(1)}, bf16[1024,512]{1,0:T(8,128)(2,1)}, u32[]{:S(2)}) copy-start(bf16[1024,512]{1,0:T(8,128)(2,1)} %param.33) | copy-start | bytes 3145732
  7.2 58.2 %all-gather.6.cloned.1.call-start = ((), (), s32[]{:S(2)}) async-start(), calls=%async_computation.3 | async-start | bytes 4456448 | tf_op jit(solution)/shard_map/all_gather | solution.py:150
  9.1 109.1 %all-gather.8.cloned.1.call-start = ((), (), s32[]{:S(2)}) async-start(), calls=%async_computation.4 | async-start | bytes 4456448 | tf_op jit(solution)/shard_map/all_gather | solution.py:151
  11.0 140.6 %reduce-scatter.4.cloned.1.call-start = ((), (), s32[]{:S(2)}) async-start(), calls=%async_computation.5 | async-start | bytes 786432 | tf_op jit(solution)/shard_map/reduce_scatter | solution.py:173
  119.5 3.0 copy-start.2
  127.6 5.4 %copy-start.8 = (bf16[1024,16]{0,1:T(8,128)(2,1)S(1)}, bf16[1024,16]{0,1:T(8,128)(2,1)}, u32[]{:S(2)}) copy-start(bf16[1024,16]{0,1:T(8,128)(2,1)} %param.30) | copy-start | bytes 98308
  127.6 10.5 %copy-start.19 = (s32[128]{0:T(128)S(1)}, s32[128]{0:T(128)}, u32[]{:S(2)}) copy-start(s32[128]{0:T(128)} %param.27) | copy-start | bytes 1540
  127.6 10.5 %copy-start.21 = (f32[8,16]{1,0:T(8,128)S(1)}, f32[8,16]{1,0:T(8,128)}, u32[]{:S(2)}) copy-start(f32[8,16]{1,0:T(8,128)} %param.32) | copy-start | bytes 1540
  127.7 23.9 %copy-start.4 = (bf16[128,1024]{1,0:T(8,128)(2,1)S(1)}, bf16[128,1024]{1,0:T(8,128)(2,1)}, u32[]{:S(2)}) copy-start(bf16[128,1024]{1,0:T(8,128)(2,1)} %param.28) | copy-start | bytes 786436
  127.7 23.9 %copy-start.5 = (bf16[16,1024]{1,0:T(8,128)(2,1)S(1)}, bf16[16,1024]{1,0:T(8,128)(2,1)}, u32[]{:S(2)}) copy-start(bf16[16,1024]{1,0:T(8,128)(2,1)} %param.31) | copy-start | bytes 98308
  127.9 26.5 %copy-start.13 = (bf16[8,512]{1,0:T(8,128)(2,1)S(1)}, bf16[8,512]{1,0:T(8,128)(2,1)}, u32[]{:S(2)}) copy-start(bf16[8,512]{1,0:T(8,128)(2,1)} %param.36) | copy-start | bytes 24580
  128.0 26.7 %copy-start.22 = (f32[8,16]{1,0:T(8,128)S(1)}, f32[8,16]{1,0:T(8,128)}, u32[]{:S(2)}) copy-start(f32[8,16]{1,0:T(8,128)} %param.42) | copy-start | bytes 1540
  131.8 42.6 %all-gather.10.cloned.1.call-start = ((), (), s32[]{:S(2)}) async-start(), calls=%async_computation.7 | async-start | bytes 1572864 | tf_op jit(solution)/shard_map/all_gather | solution.py:201
  132.3 81.9 %all-gather.12.cloned.1.call-start = ((), (), s32[]{:S(2)}) async-start(), calls=%async_computation.8 | async-start | bytes 1114112 | tf_op jit(solution)/shard_map/all_gather | solution.py:185
  132.9 103.9 %all-reduce.6.cloned.1.call-start = ((), (), s32[]{:S(2)}) async-start(), calls=%async_computation.6 | async-start | bytes 262144 | tf_op jit(solution)/shard_map/psum | solution.py:188
  138.1 80.8 %copy-start.15 = (f32[128,16]{0,1:T(8,128)}, f32[128,16]{0,1:T(8,128)S(1)}, u32[]{:S(2)}) copy-start(f32[128,16]{0,1:T(8,128)S(1)} %psum.77) | copy-start | bytes 24580
  139.0 15.6 %copy-start.10 = (bf16[128,16]{0,1:T(8,128)(2,1)}, bf16[128,16]{0,1:T(8,128)(2,1)S(1)}, u32[]{:S(2)}) copy-start(bf16[128,16]{0,1:T(8,128)(2,1)S(1)} %get-tuple-element.363) | copy-start | bytes 12292
  153.7 123.2 %all-gather.14.cloned.1.call-start = ((), (), s32[]{:S(2)}) async-start(), calls=%async_computation.9 | async-start | bytes 1114112 | tf_op jit(solution)/shard_map/all_gather | solution.py:184
  154.4 140.0 %reduce-scatter.8.cloned.1.call-start = ((), (), s32[]{:S(2)}) async-start(), calls=%async_computation.11 | async-start | bytes 49152 | tf_op jit(solution)/shard_map/reduce_scatter | solution.py:218
  154.7 64.3 %copy-start.12 = (s32[1024]{0:T(1024)}, s32[1024]{0:T(1024)S(1)}, u32[]{:S(2)}) copy-start(s32[1024]{0:T(1024)S(1)} %eq.32) | copy-start | bytes 12292
  155.2 84.8 %copy-start.17 = (f32[512]{0:T(512)S(1)}, f32[512]{0:T(512)}, u32[]{:S(2)}) copy-start(f32[512]{0:T(512)} %param.37) | copy-start | bytes 6148
  218.9 22.3 %copy-start.6 = (bf16[512,16]{0,1:T(8,128)(2,1)S(1)}, bf16[512,16]{0,1:T(8,128)(2,1)}, u32[]{:S(2)}) copy-start(bf16[512,16]{0,1:T(8,128)(2,1)} %param.40) | copy-start | bytes 49156
  239.4 0.6 copy-start.9
  240.3 1.0 copy-start.3
  276.9 3.0 copy-start.7
  276.9 3.0 copy-start.23
  282.1 1.4 copy-start.1
  284.8 31.8 %reduce-scatter.6.cloned.1.call-start = ((), (), s32[]{:S(2)}) async-start(), calls=%async_computation.10 | async-start | bytes 1572864 | tf_op jit(solution)/shard_map/reduce_scatter | solution.py:212
  289.1 138.2 %all-reduce.8.cloned.1.call-start = ((), (), s32[]{:S(2)}) async-start(), calls=%async_computation.12 | async-start | bytes 393216 | tf_op jit(solution)/shard_map/psum | solution.py:243
  316.5 8.8 %copy-start.11 = (bf16[128,16]{0,1:T(8,128)(2,1)S(1)}, bf16[128,16]{0,1:T(8,128)(2,1)}, u32[]{:S(2)}) copy-start(bf16[128,16]{0,1:T(8,128)(2,1)} %copy-done.10) | copy-start | bytes 12292
  318.1 8.1 %copy-start.18 = (f32[8,16]{1,0:T(8,128)S(1)}, f32[8,16]{1,0:T(8,128)}, u32[]{:S(2)}) copy-start(f32[8,16]{1,0:T(8,128)} %fusion.43) | copy-start | bytes 1540
  318.1 15.6 %copy-start.14 = (f32[128,16]{0,1:T(8,128)S(1)}, f32[128,16]{0,1:T(8,128)}, u32[]{:S(2)}) copy-start(f32[128,16]{0,1:T(8,128)} %get-tuple-element.364) | copy-start | bytes 24580
  318.1 16.5 %copy-start.16 = (f32[128,16]{0,1:T(8,128)S(1)}, f32[128,16]{0,1:T(8,128)}, u32[]{:S(2)}) copy-start(f32[128,16]{0,1:T(8,128)} %copy-done.15) | copy-start | bytes 24580
  318.1 16.5 %copy-start.20 = (s32[128]{0:T(128)S(1)}, s32[128]{0:T(128)}, u32[]{:S(2)}) copy-start(s32[128]{0:T(128)} %param.27) | copy-start | bytes 1540
Sparse Core Ops, SparseCore 0:
  10.1 55.1 all-gather.5
  67.5 50.6 all-gather.7
  131.9 19.6 reduce-scatter.3
  153.0 21.2 all-gather.9
  176.3 37.8 all-gather.11
  216.3 20.4 all-reduce.5
  239.0 37.8 all-gather.13
  284.9 8.9 reduce-scatter.7
  296.1 20.3 reduce-scatter.5
  334.6 92.6 all-reduce.7
